TPU v7x, 32 devices: a whole 2x2x4 slice. The times are simulated.
32 devices in a mesh: dp: 8 (over z, x), mp: 4 (over y, core).
Axes of the slice: x: 2, y: 2, z: 4, core: 2. Of those that a mesh axis runs over, the one named last changes fastest.
Arguments:
- gradients: bfloat16 [8, 3584, 14336], P(None, 'dp', 'mp'), may hold values from -60 to 60
- column_slot: int32 [8, 16], replicated, may hold values from 0 to 31, as said below
- left_roots: bfloat16 [32, 4, 4, 896, 896], P('dp', 'mp'), may hold values from -1 to 5
- right_roots: bfloat16 [32, 4, 4, 896, 896], P('dp', 'mp'), may hold values from -1 to 5
Outputs:
- update: bfloat16 [8, 3584, 14336], P(None, 'dp', 'mp')
- clip_scale: float32 [], replicated
Inputs may be any that keep to these rules, and one draw needn't show every extreme that they name: `column_slot`: block column c belongs to group c // 4; over all matrices, the entries of one group's block columns are a permutation of 0 to 31.
All inputs are finite; a program needn't handle non-finite values.
Results may differ from a plain program's by a relative error of at most 0.0049.
Values may be sent and summed in bfloat16 or wider, within the bound.
A program may use at most 256 MiB of HBM per device.

v0:
```python
import jax
import jax.numpy as jnp
from jax import lax
from jax.sharding import PartitionSpec as P

D = 3584
FF = 14336
BLOCK = 896
MATRICES = 8
rms_limit = 0.25
epsilon = 1e-06


def body(gradients, column_slot, left_roots, right_roots):
    row_count = gradients.shape[1]
    local_cols = gradients.shape[2] // BLOCK
    slot_count = MATRICES * local_cols
    mp_index = lax.axis_index("mp")
    my_slots = lax.dynamic_slice_in_dim(column_slot, mp_index * local_cols, local_cols, 1).reshape(
        slot_count
    )
    columns = (
        gradients.reshape(MATRICES, row_count, local_cols, BLOCK)
        .transpose(0, 2, 1, 3)
        .reshape(slot_count, row_count, BLOCK)
    )
    send_order = jnp.argsort(my_slots)
    ordered = jnp.take(columns, send_order, axis=0)
    owned_cols = lax.all_to_all(ordered, "dp", split_axis=0, concat_axis=1, tiled=True)
    square_sum = lax.psum(jnp.sum(jnp.square(gradients.astype(jnp.float32))), ("dp", "mp"))
    clip_scale = jnp.minimum(
        jnp.float32(1.0), rms_limit / jnp.sqrt(square_sum / (MATRICES * D * FF) + epsilon)
    )
    owned_count = owned_cols.shape[0]
    owned_blocks = owned_cols.reshape(owned_count, D // BLOCK, BLOCK, BLOCK)
    left_root = left_roots[:, 0]
    right_root = right_roots[:, 0]
    first_product = jnp.einsum(
        "snab,snbc->snac", left_root, owned_blocks, preferred_element_type=jnp.float32
    )
    scaled = (clip_scale * first_product).astype(jnp.bfloat16)
    second_product = jnp.einsum(
        "snab,snbc->snac", scaled, right_root, preferred_element_type=jnp.float32
    )
    finished = second_product.astype(jnp.bfloat16).reshape(owned_count, D, BLOCK)
    returned = lax.all_to_all(finished, "dp", split_axis=1, concat_axis=0, tiled=True)
    restored = jnp.take(returned, my_slots, axis=0)
    update = (
        restored.reshape(MATRICES, local_cols, row_count, BLOCK)
        .transpose(0, 2, 1, 3)
        .reshape(MATRICES, row_count, local_cols * BLOCK)
    )
    return (update, clip_scale)


def solution(mesh):
    return jax.shard_map(
        body,
        mesh=mesh,
        in_specs=(
            P(None, "dp", "mp"),
            P(),
            P("dp", "mp", None, None, None),
            P("dp", "mp", None, None, None),
        ),
        out_specs=(P(None, "dp", "mp"), P()),
        check_vma=False,
    )
```

profile of v0, /device:TPU:0, one launch (start us, length us, event | category | flops | bytes accessed | tf_op | source)
XLA Modules:
  0.0 1468.3 jit_solution(521979596373554846)
XLA Ops:
  0.6 0.0 copy-start
  0.7 0.7 copy-done
  1.3 0.1 constant_dynamic-slice_fusion
  1.4 0.1 reshape.30
  1.5 0.0 copy-start.2
  1.5 1.6 sort.17
  3.1 0.0 copy-done.2
  3.1 17.6 %fusion.8 = (bf16[8,448,896]{2,1,0:T(8,128)(2,1)}, bf16[8,448,896]{2,1,0:T(8,128)(2,1)}, bf16[8,448,896]{2,1,0:T(8,128)(2,1)}, bf16[8,448,896]{2,1,0:T(8,128)(2,1)}) fusion(bf16[8,448,3584]{2,1,0:T(8,128)(2,1)} %param.6), kind=kLoop, calls=%fused_computation.18 | loop fusion | bytes 51380224 | tf_op jit(solution)/shard_map/slice
  20.8 18.6 %pad_maximum_fusion = bf16[8,1792,896]{2,1,0:T(8,128)(2,1)} fusion(bf16[8,448,896]{2,1,0:T(8,128)(2,1)} %get-tuple-element.7, bf16[8,448,896]{2,1,0:T(8,128)(2,1)} %get-tuple-element.8, bf16[8,448,896]{2,1,0:T(8,128)(2,1)} %get-tuple-element.6, bf16[8,448,896]{2,1,0:T(8,128)(2,1)} %get-tuple-element.5), kind=kLoop, calls=%fused_computation.4 | loop fusion | flops 102760448 | bytes 51380224 | tf_op jit(solution)/shard_map/concatenate
  39.4 18.9 %gather_fusion = bf16[32,448,896]{2,1,0:T(8,128)(2,1)} fusion(bf16[32,448,896]{2,1,0:T(8,128)(2,1)} %bitcast.34, s32[1024]{0:T(1024)S(1)} %pad_clamp_fusion.1), kind=kCustom, calls=%fused_computation.clone | custom fusion | bytes 51380352 | tf_op jit(solution)/shard_map/jit(_take)/gather | solution.py:28
  58.3 21.6 %broadcast_select_fusion.1 = bf16[32,448,896]{2,1,0:T(8,128)(2,1)} fusion(bf16[32,448,896]{2,1,0:T(8,128)(2,1)} %gather_fusion, pred[32]{0:T(512)(128)(4,1)S(1)} %compare_and_fusion.1), kind=kLoop, calls=%fused_computation.9 | loop fusion | flops 12845056 | bytes 51380256 | tf_op jit(solution)/shard_map/jit(_take)/select_n | solution.py:28
  79.8 7.3 all-to-all-start
  87.1 15.9 %multiply_reduce_fusion = f32[]{:T(128)} fusion(bf16[8,448,3584]{2,1,0:T(8,128)(2,1)} %param.6), kind=kLoop, calls=%fused_computation.3 | loop fusion | flops 38535168 | bytes 25690116 | tf_op jit(solution)/shard_map/reduce_sum | solution.py:30
  103.0 559.1 %psum.7 = f32[]{:T(128)} all-reduce(f32[]{:T(128)} %multiply_reduce_fusion), channel_id=1, replica_groups=mesh['dp'=8,'mp'=4] {'dp','mp'}, use_global_device_ids=true, to_apply=%region_1.2 | all-reduce | flops 1 | bytes 8 | tf_op jit(solution)/shard_map/psum | solution.py:30
  662.8 0.0 all-to-all-done
  662.8 21.0 %copy.11 = bf16[4,8,448,896]{3,2,1,0:T(8,128)(2,1)} copy(bf16[4,8,448,896]{3,2,0,1:T(8,128)(2,1)} %bitcast.2) | data formatting | bytes 51380224 | tf_op jit(solution)/shard_map/all_to_all | solution.py:29
  683.8 43.5 %multiply_convert_fusion.clone.4 = bf16[4,4,896,896]{3,2,1,0:T(8,128)(2,1)} fusion(bf16[4,4,896,896]{3,2,1,0:T(8,128)(2,1)} %bitcast.39, bf16[4,1,4,896,896]{4,3,2,1,0:T(8,128)(2,1)} %param.8, f32[]{:T(128)} %min_shard_map.3), kind=kOutput, calls=%fused_computation.2.clone.clone.clone.1 | convolution fusion | flops 23044030464 | bytes 77070336 | tf_op jit(solution)/shard_map/snab,snbc->snac/dot_general | solution.py:38
  727.3 43.5 %fusion.3 = bf16[4,4,896,896]{3,2,1,0:T(8,128)(2,1)} fusion(bf16[4,1,4,896,896]{4,3,2,1,0:T(8,128)(2,1)} %param.9, bf16[4,4,896,896]{3,2,1,0:T(8,128)(2,1)} %multiply_convert_fusion.clone.4), kind=kOutput, calls=%fused_computation.10 | convolution fusion | flops 23031185408 | bytes 77070336 | tf_op jit(solution)/shard_map/snab,snbc->snac/dot_general | solution.py:42
  770.8 56.9 %copy.14 = bf16[4,3584,896]{2,0,1:T(4,128)(2,1)} copy(bf16[4,3584,896]{2,1,0:T(8,128)(2,1)} %bitcast.40) | data formatting | bytes 51380224 | tf_op jit(solution)/shard_map/reshape | solution.py:45
  827.7 0.0 copy-start.3
  827.7 6.5 all-to-all-start.1
  834.2 0.0 copy-done.3
  834.2 553.4 %all-to-all-done.1 = bf16[4,3584,896]{2,0,1:T(4,128)(2,1)} async-done(((bf16[4,3584,896]{2,0,1:T(4,128)(2,1)}), bf16[4,3584,896]{2,0,1:T(4,128)(2,1)}, u32[]{:S(2)}, u32[]{:S(2)}) %all-to-all-start.1) | async-done | bytes 25690144 | tf_op jit(solution)/shard_map/all_to_all | solution.py:46
  1387.7 17.5 %copy.15 = bf16[4,3584,896]{2,1,0:T(8,128)(2,1)} copy(bf16[4,3584,896]{2,0,1:T(4,128)(2,1)} %all-to-all-done.1) | data formatting | bytes 51380224 | tf_op jit(solution)/shard_map/all_to_all | solution.py:46
  1405.2 21.0 %copy.16 = bf16[8,4,448,896]{3,2,1,0:T(8,128)(2,1)} copy(bf16[8,4,448,896]{3,2,0,1:T(8,128)(2,1)} %bitcast.37) | data formatting | bytes 51380224 | tf_op jit(solution)/shard_map/all_to_all | solution.py:46
  1426.2 19.2 %gather_fusion.1 = bf16[32,448,896]{2,1,0:T(8,128)(2,1)} fusion(bf16[32,448,896]{2,1,0:T(8,128)(2,1)} %bitcast.35, s32[1024]{0:T(1024)S(1)} %pad_clamp_fusion), kind=kCustom, calls=%fused_computation.1.clone | custom fusion | bytes 51380352 | tf_op jit(solution)/shard_map/jit(_take)/gather | solution.py:47
  1445.4 12.9 broadcast_select_fusion
  1458.3 0.0 copy-start.1
  1458.3 8.8 copy.20
  1467.1 0.0 copy-done.1
  (7 shorter events, 0.0 us)
Async XLA Ops:
  0.6 0.7 copy-start
  1.5 1.6 copy-start.2
  79.8 583.0 %all-to-all-start = ((bf16[32,448,896]{2,1,0:T(8,128)(2,1)}), bf16[32,448,896]{2,1,0:T(8,128)(2,1)}, u32[]{:S(2)}, u32[]{:S(2)}) async-start(bf16[32,448,896]{2,1,0:T(8,128)(2,1)} %broadcast_select_fusion.1), calls=%async_computation | async-start | bytes 51380224 | tf_op jit(solution)/shard_map/all_to_all | solution.py:29
  827.7 6.5 copy-start.3
  827.7 560.0 %all-to-all-start.1 = ((bf16[4,3584,896]{2,0,1:T(4,128)(2,1)}), bf16[4,3584,896]{2,0,1:T(4,128)(2,1)}, u32[]{:S(2)}, u32[]{:S(2)}) async-start(bf16[4,3584,896]{2,0,1:T(4,128)(2,1)} %copy.14), calls=%async_computation.1 | async-start | bytes 51380224 | tf_op jit(solution)/shard_map/all_to_all | solution.py:46
  1458.3 8.8 copy-start.1
where the time goes:
time: 1470 us
  blocking collectives  559 us (38%)
  waiting for transfers between devices  553 us (38%)
  local copies, waits for them, and re-layouts  182 us (12%)
  matrix products  87 us (6%)
  other arithmetic  70.6 us (5%)
    psum x1, blocking collectives, body(): lax.psum(jnp.sum(jnp.square(gradients.astype(jnp.float32))), ('dp', 'mp'))  559 us
    all_to_all x1, waiting for transfers between devices, body(): lax.all_to_all(finished, 'dp', split_axis=1, concat_axis=0, tiled=True)  553 us
    reshape x1, local copies, waits for them, and re-layouts, body(): second_product.astype(jnp.bfloat16).reshape(owned_count, D, BLOCK)  56.9 us
    dot_general x1, matrix products, body(): jnp.einsum('snab,snbc->snac', scaled, right_root, preferred_element_type=...  43.5 us
    dot_general x1, matrix products, body(): jnp.einsum('snab,snbc->snac', left_root, owned_blocks, preferred_element_...  43.5 us
    all_to_all x2, local copies, waits for them, and re-layouts, body(): lax.all_to_all(finished, 'dp', split_axis=1, concat_axis=0, tiled=True)  38.5 us
  transfers between devices with their start and end apart: 2, of which 1 were waited for; matrix products, arithmetic and copies ran while one was open for 1% of the time, Pallas kernels for 0%

commit v1 on v0

--- a/solution.py
+++ b/solution.py
@@ -9,6 +9,12 @@
 MATRICES = 8
 rms_limit = 0.25
 epsilon = 1e-06
+
+
+def trade_parts(array, axis, split, join):
+    parts = jnp.split(array, lax.axis_size(axis), axis=split)
+    received = lax.all_to_all(jnp.stack(parts), axis, 0, 0)
+    return jnp.concatenate(received, axis=join)
 
 
 def body(gradients, column_slot, left_roots, right_roots):
@@ -43,7 +49,7 @@
         "snab,snbc->snac", scaled, right_root, preferred_element_type=jnp.float32
     )
     finished = second_product.astype(jnp.bfloat16).reshape(owned_count, D, BLOCK)
-    returned = lax.all_to_all(finished, "dp", split_axis=1, concat_axis=0, tiled=True)
+    returned = trade_parts(finished, "dp", 1, 0)
     restored = jnp.take(returned, my_slots, axis=0)
     update = (
         restored.reshape(MATRICES, local_cols, row_count, BLOCK)

time: 1470 us -> 1400 us (0.952)
  local copies, waits for them, and re-layouts: 182 us -> 112 us
    reshape x1 -> x0, local copies, waits for them, and re-layouts: 56.9 us -> none  [body(): second_product.astype(jnp.bfloat16).reshape(owned_count, D, BLOCK)]
    all_to_all x2 -> x0, local copies, waits for them, and re-layouts: 38.5 us -> none  [body(): lax.all_to_all(finished, 'dp', split_axis=1, concat_axis=0, tiled=True)]
    unnamed x8 -> x17, local copies, waits for them, and re-layouts: 0.7 us -> 24.2 us
where the time goes in v1:
time: 1400 us
  blocking collectives  559 us (40%)
  waiting for transfers between devices  553 us (40%)
  local copies, waits for them, and re-layouts  112 us (8%)
  matrix products  87 us (6%)
  other arithmetic  70.6 us (5%)
    psum x1, blocking collectives, body(): lax.psum(jnp.sum(jnp.square(gradients.astype(jnp.float32))), ('dp', 'mp'))  559 us
    all_to_all x1, waiting for transfers between devices, trade_parts(): received = lax.all_to_all(jnp.stack(parts), axis, 0, 0)  553 us
    dot_general x1, matrix products, body(): jnp.einsum('snab,snbc->snac', scaled, right_root, preferred_element_type=...  43.5 us
    dot_general x1, matrix products, body(): jnp.einsum('snab,snbc->snac', left_root, owned_blocks, preferred_element_...  43.5 us
  transfers between devices with their start and end apart: 2, of which 1 were waited for; matrix products, arithmetic and copies ran while one was open for 1% of the time, Pallas kernels for 0%

profile of v1, /device:TPU:0, one launch (start us, length us, event | category | flops | bytes accessed | tf_op | source)
XLA Modules:
  0.0 1398.4 jit_solution(988415917645018472)
XLA Ops:
  0.6 0.0 copy-start
  0.7 0.7 copy-done
  1.3 0.1 constant_dynamic-slice_fusion
  1.4 0.1 reshape.33
  1.5 0.0 copy-start.3
  1.5 1.6 sort.17
  3.1 0.0 copy-done.3
  3.1 17.6 %fusion.16 = (bf16[8,448,896]{2,1,0:T(8,128)(2,1)}, bf16[8,448,896]{2,1,0:T(8,128)(2,1)}, bf16[8,448,896]{2,1,0:T(8,128)(2,1)}, bf16[8,448,896]{2,1,0:T(8,128)(2,1)}) fusion(bf16[8,448,3584]{2,1,0:T(8,128)(2,1)} %param.6), kind=kLoop, calls=%fused_computation.34 | loop fusion | bytes 51380224 | tf_op jit(solution)/shard_map/slice
  20.8 18.6 %pad_maximum_fusion = bf16[8,1792,896]{2,1,0:T(8,128)(2,1)} fusion(bf16[8,448,896]{2,1,0:T(8,128)(2,1)} %get-tuple-element.7, bf16[8,448,896]{2,1,0:T(8,128)(2,1)} %get-tuple-element.8, bf16[8,448,896]{2,1,0:T(8,128)(2,1)} %get-tuple-element.6, bf16[8,448,896]{2,1,0:T(8,128)(2,1)} %get-tuple-element.5), kind=kLoop, calls=%fused_computation.4 | loop fusion | flops 102760448 | bytes 51380224 | tf_op jit(solution)/shard_map/concatenate
  39.4 18.9 %gather_fusion = bf16[32,448,896]{2,1,0:T(8,128)(2,1)} fusion(bf16[32,448,896]{2,1,0:T(8,128)(2,1)} %bitcast.63, s32[1024]{0:T(1024)S(1)} %pad_clamp_fusion.1), kind=kCustom, calls=%fused_computation.clone | custom fusion | bytes 51380352 | tf_op jit(solution)/shard_map/jit(_take)/gather | solution.py:34
  58.3 21.6 %broadcast_select_fusion.1 = bf16[32,448,896]{2,1,0:T(8,128)(2,1)} fusion(bf16[32,448,896]{2,1,0:T(8,128)(2,1)} %gather_fusion, pred[32]{0:T(512)(128)(4,1)S(1)} %compare_and_fusion.1), kind=kLoop, calls=%fused_computation.9 | loop fusion | flops 12845056 | bytes 51380256 | tf_op jit(solution)/shard_map/jit(_take)/select_n | solution.py:34
  79.8 7.3 all-to-all-start
  87.1 15.9 %multiply_reduce_fusion = f32[]{:T(128)} fusion(bf16[8,448,3584]{2,1,0:T(8,128)(2,1)} %param.6), kind=kLoop, calls=%fused_computation.3 | loop fusion | flops 38535168 | bytes 25690116 | tf_op jit(solution)/shard_map/reduce_sum | solution.py:36
  103.0 559.1 %psum.7 = f32[]{:T(128)} all-reduce(f32[]{:T(128)} %multiply_reduce_fusion), channel_id=1, replica_groups=mesh['dp'=8,'mp'=4] {'dp','mp'}, use_global_device_ids=true, to_apply=%region_1.2 | all-reduce | flops 1 | bytes 8 | tf_op jit(solution)/shard_map/psum | solution.py:36
  662.8 0.0 all-to-all-done
  662.8 21.0 %copy.6 = bf16[4,8,448,896]{3,2,1,0:T(8,128)(2,1)} copy(bf16[4,8,448,896]{3,2,0,1:T(8,128)(2,1)} %bitcast.2) | data formatting | bytes 51380224 | tf_op jit(solution)/shard_map/all_to_all | solution.py:35
  683.8 43.5 %multiply_convert_fusion.clone.4 = bf16[4,4,896,896]{3,2,1,0:T(8,128)(2,1)} fusion(bf16[4,4,896,896]{3,2,1,0:T(8,128)(2,1)} %bitcast.74, bf16[4,1,4,896,896]{4,3,2,1,0:T(8,128)(2,1)} %param.8, f32[]{:T(128)} %min_shard_map.3), kind=kOutput, calls=%fused_computation.2.clone.clone.clone.1 | convolution fusion | flops 23044030464 | bytes 77070336 | tf_op jit(solution)/shard_map/snab,snbc->snac/dot_general | solution.py:44
  727.3 43.5 %fusion.3 = bf16[4,4,896,896]{3,2,1,0:T(8,128)(2,1)} fusion(bf16[4,1,4,896,896]{4,3,2,1,0:T(8,128)(2,1)} %param.9, bf16[4,4,896,896]{3,2,1,0:T(8,128)(2,1)} %multiply_convert_fusion.clone.4), kind=kOutput, calls=%fused_computation.10 | convolution fusion | flops 23031185408 | bytes 77070336 | tf_op jit(solution)/shard_map/snab,snbc->snac/dot_general | solution.py:48
  770.8 0.0 copy-start.2
  770.9 4.0 fusion.13
  774.8 4.6 fusion.12
  779.5 4.6 fusion.11
  784.0 4.4 fusion.10
  788.4 0.0 copy-done.2
  788.4 1.9 fusion.9
  790.3 2.0 fusion.8
  792.3 2.0 fusion.7
  794.3 1.9 fusion.6
  796.2 0.0 copy-start.4
  796.2 6.6 all-to-all-start.1
  802.8 0.0 copy-done.4
  802.9 553.4 %all-to-all-done.1 = bf16[8,4,448,896]{3,2,1,0:T(8,128)(2,1)} async-done(((bf16[8,4,448,896]{3,2,1,0:T(8,128)(2,1)}), bf16[8,4,448,896]{3,2,1,0:T(8,128)(2,1)}, u32[]{:S(2)}, u32[]{:S(2)}) %all-to-all-start.1) | async-done | bytes 25690144 | tf_op jit(solution)/shard_map/all_to_all | solution.py:16
  1356.3 19.2 %gather_fusion.1 = bf16[32,448,896]{2,1,0:T(8,128)(2,1)} fusion(bf16[32,448,896]{2,1,0:T(8,128)(2,1)} %bitcast.15, s32[1024]{0:T(1024)S(1)} %pad_clamp_fusion), kind=kCustom, calls=%fused_computation.1.clone | custom fusion | bytes 51380352 | tf_op jit(solution)/shard_map/jit(_take)/gather | solution.py:53
  1375.5 12.9 broadcast_select_fusion
  1388.4 0.0 copy-start.1
  1388.4 8.8 copy.12
  1397.2 0.0 copy-done.1
  (7 shorter events, 0.0 us)
Async XLA Ops:
  0.6 0.7 copy-start
  1.5 1.6 copy-start.3
  79.8 583.0 %all-to-all-start = ((bf16[32,448,896]{2,1,0:T(8,128)(2,1)}), bf16[32,448,896]{2,1,0:T(8,128)(2,1)}, u32[]{:S(2)}, u32[]{:S(2)}) async-start(bf16[32,448,896]{2,1,0:T(8,128)(2,1)} %broadcast_select_fusion.1), calls=%async_computation | async-start | bytes 51380224 | tf_op jit(solution)/shard_map/all_to_all | solution.py:35
  770.8 17.6 %copy-start.2 = (bf16[4,4,896,896]{3,2,1,0:T(8,128)(2,1)S(1)}, bf16[4,4,896,896]{3,2,1,0:T(8,128)(2,1)}, u32[]{:S(2)}) copy-start(bf16[4,4,896,896]{3,2,1,0:T(8,128)(2,1)} %fusion.3) | copy-start | bytes 77070336
  796.2 6.6 copy-start.4
  796.2 560.1 %all-to-all-start.1 = ((bf16[8,4,448,896]{3,2,1,0:T(8,128)(2,1)}), bf16[8,4,448,896]{3,2,1,0:T(8,128)(2,1)}, u32[]{:S(2)}, u32[]{:S(2)}) async-start(bf16[8,4,448,896]{3,2,1,0:T(8,128)(2,1)} %fusion.6), calls=%async_computation.1 | async-start | bytes 51380224 | tf_op jit(solution)/shard_map/all_to_all | solution.py:16
  1388.4 8.8 copy-start.1
